TPU v7x, 128 devices: a whole 4x4x4 slice. The times are simulated.
128 devices in a mesh: vocab: 128 (over y, z, x, core).
Axes of the slice: x: 4, y: 4, z: 4, core: 2. Of those that a mesh axis runs over, the one named last changes fastest.
Arguments:
- draft_ids: int32 [128, 8], P('vocab'), may hold values from 0 to 262143, as said below
- draft_len: int32 [128], P('vocab'), may hold values from 1 to 8
- accepted: int32 [128], P('vocab'), may hold values from 1 to 8
- targets: int32 [128, 8], P('vocab'), may hold values from 0 to 262143
- hidden: bfloat16 [128, 8, 2048], P('vocab'), may hold values from -6 to 6
- ple_table: bfloat16 [262144, 512], P('vocab'), may hold values from -6 to 6
- gate_proj: bfloat16 [2, 2048, 256], replicated, may hold values from -0.125 to 0.125
- out_proj: bfloat16 [2, 256, 2048], replicated, may hold values from -0.375 to 0.375
- post_gain: float32 [2, 2048], replicated, may hold values from 0.25 to 1.75
- final_gain: float32 [2048], replicated, may hold values from 0.25 to 1.75
- embedding: bfloat16 [262144, 2048], P('vocab'), may hold values from -0.44921875 to 0.44921875
Outputs:
- token_logprob: float32 [128, 8], P('vocab')
- seq_logprob: float32 [128], P('vocab')
Inputs may be any that keep to these rules, and one draw needn't show every extreme that they name: `draft_ids`: among the 8 draft ids of one device's sequences, at most 2 lie in any one aligned block of 2048 vocabulary entries, and in every draw some block holds exactly 2 of them.
All inputs are finite; a program needn't handle non-finite values.
Results may differ from a plain program's by a relative error of at most 0.00096.
Values may be sent and summed in bfloat16 or wider, within the bound.
A program may use at most 64 MiB of HBM per device.

v0:
```python
import jax
import jax.numpy as jnp
from jax import lax
from jax.sharding import Mesh
from jax.sharding import PartitionSpec as P

MOST = 2
VOCAB = ("vocab_0", "vocab_1", "vocab_2", "vocab_3")


def copy_for_each(value, axis):
    length = lax.axis_size(axis)
    return lax.all_to_all(
        jnp.broadcast_to(value[None], (length, *value.shape)), axis, 0, 0, tiled=True
    )


def joined_along(tiles, dim):
    tiles = jnp.moveaxis(tiles, 0, dim)
    lengths = tiles.shape
    return tiles.reshape(*lengths[:dim], lengths[dim] * lengths[dim + 1], *lengths[dim + 2 :])


def gather_axes(value, axes, dim):
    far, near = axes
    tiles = copy_for_each(copy_for_each(value, far), near)
    return joined_along(tiles.swapaxes(0, 1).reshape(-1, *value.shape), dim)


def collected_together(value, axis):
    leaves = jax.tree.leaves(value)
    order = sorted(range(len(leaves)), key=lambda k: -leaves[k].size)
    width = (1, *leaves[order[0]].shape)[-1]
    lines = [
        jnp.pad(leaves[k].reshape(-1), (0, -leaves[k].size % width)).reshape(-1, width)
        for k in order
    ]
    both, at, found = (lax.all_gather(jnp.concatenate(lines), axis), 0, {})
    for k, line in zip(order, lines):
        slab = both[:, at : at + len(line)].reshape(len(both), -1)
        found[k] = slab[:, : leaves[k].size].reshape(-1, *leaves[k].shape)
        at += len(line)
    numbers = iter(range(len(leaves)))
    return jax.tree.map(lambda _: found[next(numbers)], value)


def combined_by_axis(value, axes, combine):
    for axis in axes:
        pieces = collected_together(value, axis)
        value = jax.tree.map(lambda part: part[0], pieces)
        for k in range(1, lax.axis_size(axis)):
            value = combine(value, jax.tree.map(lambda part: part[k], pieces))
    return value


def rms_norm(value):
    return value / jnp.sqrt(jnp.mean(value * value, axis=-1, keepdims=True) + 1e-06)


def combine(first, second):
    return (first[0] + second[0], first[1] + second[1])


def same_rank(holder):
    count = holder.shape[-1]
    earlier = lax.iota(jnp.int32, count)[:, None] > lax.iota(jnp.int32, count)[None, :]
    match = holder[..., :, None] == holder[..., None, :]
    return jnp.sum(jnp.where(earlier & match, 1, 0), axis=-1).astype(jnp.int32)


def per_device(
    draft_ids,
    draft_len,
    accepted,
    targets,
    hidden,
    ple_table,
    gate_proj,
    out_proj,
    post_gain,
    final_gain,
    embedding,
):
    seq_dev, draft = draft_ids.shape
    tok_dev = seq_dev * draft
    voc_dev, ple_width = ple_table.shape
    width = hidden.shape[2]
    owner = lax.axis_index(VOCAB)
    columns = owner * voc_dev + lax.iota(jnp.int32, voc_dev)
    all_ids = gather_axes(
        draft_ids.reshape(tok_dev), (("vocab_0", "vocab_1", "vocab_2"), "vocab_3"), 0
    )
    everyone = all_ids.shape[0]
    members = everyone // tok_dev
    id_grid = all_ids.reshape(members, tok_dev)
    holder = id_grid // voc_dev
    mine_hit = holder == owner
    rank = same_rank(holder)
    slot_index = lax.iota(jnp.int32, MOST)
    select = mine_hit[:, None, :] & (rank[:, None, :] == slot_index[None, :, None])
    within = jnp.sum(jnp.where(select, id_grid[:, None, :] - owner * voc_dev, 0), axis=2)
    filled = jnp.any(select, axis=2)
    onehot = (
        filled[:, :, None] & (within[:, :, None] == lax.iota(jnp.int32, voc_dev)[None, None, :])
    ).astype(jnp.bfloat16)
    packed = jnp.dot(
        onehot.reshape(members * MOST, voc_dev), ple_table, preferred_element_type=jnp.float32
    )
    packed = packed.astype(jnp.bfloat16).reshape(members, MOST, ple_width)
    arrived = lax.all_to_all(packed, VOCAB, split_axis=0, concat_axis=0, tiled=True)
    own_ids = draft_ids.reshape(tok_dev)
    own_holder = own_ids // voc_dev
    own_rank = same_rank(own_holder)
    flat_slot = own_holder * MOST + own_rank
    picker = (flat_slot[:, None] == lax.iota(jnp.int32, members * MOST)[None, :]).astype(
        jnp.bfloat16
    )
    rows = jnp.dot(
        picker, arrived.reshape(members * MOST, ple_width), preferred_element_type=jnp.float32
    )
    place = lax.iota(jnp.int32, draft)[None, :]
    live = (place < draft_len[:, None]).reshape(tok_dev, 1)
    ple = jnp.where(live, rows, 0.0).astype(jnp.bfloat16)
    state = hidden.reshape(tok_dev, width)
    inner = gate_proj.shape[2]
    for layer in range(gate_proj.shape[0]):
        gated = jax.nn.gelu(
            jnp.dot(state, gate_proj[layer], preferred_element_type=jnp.float32), approximate=True
        )
        gated = (gated * ple[:, layer * inner : (layer + 1) * inner].astype(jnp.float32)).astype(
            jnp.bfloat16
        )
        branch = jnp.dot(gated, out_proj[layer], preferred_element_type=jnp.float32)
        state = (state.astype(jnp.float32) + post_gain[layer] * rms_norm(branch)).astype(
            jnp.bfloat16
        )
    normed = (final_gain * rms_norm(state.astype(jnp.float32))).astype(jnp.bfloat16)
    states = gather_axes(normed, (("vocab_0", "vocab_1", "vocab_2"), "vocab_3"), 0)
    wanted = gather_axes(
        targets.reshape(tok_dev), (("vocab_0", "vocab_1", "vocab_2"), "vocab_3"), 0
    )
    logits = lax.dot_general(
        states, embedding, (((1,), (1,)), ((), ())), preferred_element_type=jnp.float32
    )
    logits = 30.0 * jnp.tanh(logits / 30.0)
    total = jnp.sum(jnp.exp(logits), axis=1)
    picked = jnp.sum(jnp.where(columns[None, :] == wanted[:, None], logits, 0.0), axis=1)
    local = (total, picked)
    total, picked = combined_by_axis(local, VOCAB, combine)
    mine = owner * tok_dev
    total = lax.dynamic_slice_in_dim(total, mine, tok_dev)
    picked = lax.dynamic_slice_in_dim(picked, mine, tok_dev)
    logprob = (picked - jnp.log(total)).reshape(seq_dev, draft)
    keep = place < jnp.minimum(accepted, draft_len)[:, None]
    token_logprob = jnp.where(keep, logprob, 0.0)
    return (token_logprob, jnp.sum(token_logprob, axis=1))


def solution(mesh):
    finer = Mesh(mesh.devices.reshape(4, 4, 4, 2), ("vocab_0", "vocab_1", "vocab_2", "vocab_3"))
    placed = (
        P(VOCAB, None),
        P(VOCAB),
        P(VOCAB),
        P(VOCAB, None),
        P(VOCAB, None, None),
        P(VOCAB, None),
        P(),
        P(),
        P(),
        P(),
        P(VOCAB, None),
    )
    return jax.shard_map(
        per_device,
        mesh=finer,
        in_specs=placed,
        out_specs=(P(VOCAB, None), P(VOCAB)),
        check_vma=False,
    )
```

profile of v0, /device:TPU:1, one launch (start us, length us, event | category | flops | bytes accessed | tf_op | source)
XLA Modules:
  0.0 167.7 jit_solution(6232729375524544018)
XLA Ops:
  0.7 1.4 broadcast_in_dim.65
  2.1 12.0 %all-to-all-start = ((s32[64,1,8]{2,1,0:T(1,128)}), s32[64,1,8]{2,1,0:T(1,128)S(1)}, u32[]{:S(2)}, u32[]{:S(2)}) async-start(s32[64,1,8]{2,1,0:T(1,128)} %broadcast_in_dim.65), calls=%async_computation | async-start | bytes 65536 | tf_op jit(solution)/shard_map/all_to_all | solution.py:13
  17.7 4.8 %all-to-all-done = s32[64,1,8]{2,1,0:T(1,128)S(1)} async-done(((s32[64,1,8]{2,1,0:T(1,128)}), s32[64,1,8]{2,1,0:T(1,128)S(1)}, u32[]{:S(2)}, u32[]{:S(2)}) %all-to-all-start) | async-done | bytes 2080 | tf_op jit(solution)/shard_map/all_to_all | solution.py:13
  22.6 5.4 %all_to_all.37 = s32[2,1,512]{2,1,0:T(1,128)S(1)} all-to-all(s32[2,1,512]{2,1,0:T(1,128)S(1)} %reshape.560), channel_id=1, replica_groups=mesh['vocab_0'=4,'vocab_1'=4,'vocab_2'=4,'vocab_3'=2] {'vocab_3'}, dimensions={0} | all-to-all | bytes 8192 | tf_op jit(solution)/shard_map/all_to_all | solution.py:13
  28.0 1.3 broadcast_in_dim.124
  29.3 4.7 %all-to-all-start.5 = ((s32[64,1,8]{2,1,0:T(1,128)}), s32[64,1,8]{2,1,0:T(1,128)S(1)}, u32[]{:S(2)}, u32[]{:S(2)}) async-start(s32[64,1,8]{2,1,0:T(1,128)} %broadcast_in_dim.124), calls=%async_computation.5 | async-start | bytes 65536 | tf_op jit(solution)/shard_map/all_to_all | solution.py:13
  37.8 4.6 %all-to-all-done.5 = s32[64,1,8]{2,1,0:T(1,128)S(1)} async-done(((s32[64,1,8]{2,1,0:T(1,128)}), s32[64,1,8]{2,1,0:T(1,128)S(1)}, u32[]{:S(2)}, u32[]{:S(2)}) %all-to-all-start.5) | async-done | bytes 2080 | tf_op jit(solution)/shard_map/all_to_all | solution.py:13
  42.5 5.3 %all-to-all-start.2 = ((bf16[128,2,512]{2,1,0:T(2,128)(2,1)}), bf16[128,2,512]{2,1,0:T(2,128)(2,1)S(1)}, u32[]{:S(2)}, u32[]{:S(2)}) async-start(bf16[128,2,512]{2,1,0:T(2,128)(2,1)} %reshape.540), calls=%async_computation.2 | async-start | bytes 524288 | tf_op jit(solution)/shard_map/all_to_all | solution.py:110
  48.5 10.3 %all-to-all-done.2 = bf16[128,2,512]{2,1,0:T(2,128)(2,1)S(1)} async-done(((bf16[128,2,512]{2,1,0:T(2,128)(2,1)}), bf16[128,2,512]{2,1,0:T(2,128)(2,1)S(1)}, u32[]{:S(2)}, u32[]{:S(2)}) %all-to-all-start.2) | async-done | bytes 262176 | tf_op jit(solution)/shard_map/all_to_all | solution.py:110
  58.8 3.9 %all-to-all-start.6 = ((s32[2,1,512]{2,1,0:T(1,128)}), s32[2,1,512]{2,1,0:T(1,128)S(1)}, u32[]{:S(2)}, u32[]{:S(2)}) async-start(s32[2,1,512]{2,1,0:T(1,128)} %reshape.562), calls=%async_computation.6 | async-start | bytes 8192 | tf_op jit(solution)/shard_map/all_to_all | solution.py:13
  63.0 2.4 %multiply_reduce_fusion.1 = (f32[8]{0:T(128)S(1)}, f32[8,2048]{1,0:T(8,128)S(1)}) fusion(bf16[2,256,2048]{2,1,0:T(8,128)(2,1)} %param.18, bf16[2,2048,256]{2,1,0:T(8,128)(2,1)} %param.17, bf16[1,8,2048]{2,1,0:T(8,128)(2,1)S(1)} %copy-done.1, bf16[8,512]{1,0:T(8,128)(2,1)S(1)} %fusion.6), kind=kOutput, calls=%fused_computation.31 | convolution fusion | flops 16832504 | bytes 2199584 | tf_op jit(solution)/shard_map/dot_general | solution.py:133
  65.5 2.4 %multiply_reduce_fusion = (f32[8]{0:T(128)S(1)}, f32[8,2048]{1,0:T(8,128)S(1)}) fusion(bf16[2,256,2048]{2,1,0:T(8,128)(2,1)} %param.18, bf16[8,2048]{1,0:T(8,128)(2,1)S(1)} %add_convert_fusion.1, bf16[2,2048,256]{2,1,0:T(8,128)(2,1)} %param.17, bf16[8,512]{1,0:T(8,128)(2,1)S(1)} %fusion.6), kind=kOutput, calls=%fused_computation.29 | convolution fusion | flops 16832504 | bytes 2199584 | tf_op jit(solution)/shard_map/dot_general | solution.py:133
  68.3 1.5 broadcast_in_dim.122
  69.8 5.6 %all-to-all-start.3 = ((bf16[64,8,2048]{2,1,0:T(8,128)(2,1)}), bf16[64,8,2048]{2,1,0:T(8,128)(2,1)}, u32[]{:S(2)}, u32[]{:S(2)}) async-start(bf16[64,8,2048]{2,1,0:T(8,128)(2,1)} %broadcast_in_dim.122), calls=%async_computation.3 | async-start | bytes 4194304 | tf_op jit(solution)/shard_map/all_to_all | solution.py:13
  77.1 28.7 %all-to-all-done.3 = bf16[64,8,2048]{2,1,0:T(8,128)(2,1)} async-done(((bf16[64,8,2048]{2,1,0:T(8,128)(2,1)}), bf16[64,8,2048]{2,1,0:T(8,128)(2,1)}, u32[]{:S(2)}, u32[]{:S(2)}) %all-to-all-start.3) | async-done | bytes 2097184 | tf_op jit(solution)/shard_map/all_to_all | solution.py:13
  105.8 2.1 %broadcast_in_dim.123 = bf16[2,64,8,2048]{3,2,1,0:T(8,128)(2,1)S(1)} broadcast(bf16[64,8,2048]{2,1,0:T(8,128)(2,1)} %all-to-all-done.3), dimensions={1,2,3} | broadcast | bytes 6291456 | tf_op jit(solution)/shard_map/broadcast_in_dim | solution.py:14
  107.9 8.2 %all_to_all.38 = bf16[2,64,8,2048]{3,2,1,0:T(8,128)(2,1)S(1)} all-to-all(bf16[2,64,8,2048]{3,2,1,0:T(8,128)(2,1)S(1)} %broadcast_in_dim.123), channel_id=1, replica_groups=mesh['vocab_0'=4,'vocab_1'=4,'vocab_2'=4,'vocab_3'=2] {'vocab_3'}, dimensions={0} | all-to-all | bytes 8388608 | tf_op jit(solution)/shard_map/all_to_all | solution.py:13
  116.7 1.6 slice-done.1
  118.3 10.4 %exponential_reduce_fusion = (f32[1024]{0:T(1024)S(1)}, f32[1024]{0:T(1024)S(1)}) fusion(s32[1024]{0:T(1024)S(1)} %eq.115, s32[2048]{0:T(1024)S(1)} %iota_add_fusion, bf16[1024,2048]{1,0:T(8,128)(2,1)S(1)} %bitcast.112, bf16[2048,2048]{1,0:T(8,128)(2,1)S(1)} %bitcast.125), kind=kOutput, calls=%fused_computation.1 | convolution fusion | flops 8602515456 | bytes 12603392 | tf_op jit(solution)/shard_map/dot_general | solution.py:142
  128.7 9.0 %all-gather.4 = f32[4,2,1024]{2,1,0:T(2,128)S(1)} all-gather(f32[1,2,1024]{2,1,0:T(2,128)S(1)} %maximum_bitcast_fusion), channel_id=2, replica_groups=mesh['vocab_0'=4,'vocab_1'=4,'vocab_2'=4,'vocab_3'=2] {'vocab_0'}, dimensions={0}, use_global_device_ids=true | all-gather | bytes 40960 | tf_op jit(solution)/shard_map/all_gather | solution.py:38
  137.8 9.0 %all-gather.5 = f32[4,2,1024]{2,1,0:T(2,128)S(1)} all-gather(f32[1,2,1024]{2,1,0:T(2,128)S(1)} %maximum_bitcast_fusion.1), channel_id=3, replica_groups=mesh['vocab_0'=4,'vocab_1'=4,'vocab_2'=4,'vocab_3'=2] {'vocab_1'}, dimensions={0}, use_global_device_ids=true | all-gather | bytes 40960 | tf_op jit(solution)/shard_map/all_gather | solution.py:38
  146.9 9.0 %all-gather.6 = f32[4,2,1024]{2,1,0:T(2,128)S(1)} all-gather(f32[1,2,1024]{2,1,0:T(2,128)S(1)} %maximum_bitcast_fusion.2), channel_id=4, replica_groups=mesh['vocab_0'=4,'vocab_1'=4,'vocab_2'=4,'vocab_3'=2] {'vocab_2'}, dimensions={0}, use_global_device_ids=true | all-gather | bytes 40960 | tf_op jit(solution)/shard_map/all_gather | solution.py:38
  155.9 10.5 %all-gather.7 = f32[2,2,1024]{2,1,0:T(2,128)S(1)} all-gather(f32[1,2,1024]{2,1,0:T(2,128)S(1)} %maximum_bitcast_fusion.3), channel_id=5, replica_groups=mesh['vocab_0'=4,'vocab_1'=4,'vocab_2'=4,'vocab_3'=2] {'vocab_3'}, dimensions={0}, use_global_device_ids=true | all-gather | bytes 24576 | tf_op jit(solution)/shard_map/all_gather | solution.py:38
  166.5 1.2 fusion.103
  (65 shorter events, 10.1 us)
Async XLA Ops:
  0.6 35.6 %copy-start = (bf16[2048,512]{1,0:T(8,128)(2,1)S(1)}, bf16[2048,512]{1,0:T(8,128)(2,1)}, u32[]{:S(2)}) copy-start(bf16[2048,512]{1,0:T(8,128)(2,1)} %param.16) | copy-start | bytes 6291460
  0.6 62.4 %copy-start.1 = (bf16[1,8,2048]{2,1,0:T(8,128)(2,1)S(1)}, bf16[1,8,2048]{2,1,0:T(8,128)(2,1)}, u32[]{:S(2)}) copy-start(bf16[1,8,2048]{2,1,0:T(8,128)(2,1)} %param.15) | copy-start | bytes 98308
  2.1 20.4 %all-to-all-start = ((s32[64,1,8]{2,1,0:T(1,128)}), s32[64,1,8]{2,1,0:T(1,128)S(1)}, u32[]{:S(2)}, u32[]{:S(2)}) async-start(s32[64,1,8]{2,1,0:T(1,128)} %broadcast_in_dim.65), calls=%async_computation | async-start | bytes 65536 | tf_op jit(solution)/shard_map/all_to_all | solution.py:13
  29.3 13.2 %all-to-all-start.5 = ((s32[64,1,8]{2,1,0:T(1,128)}), s32[64,1,8]{2,1,0:T(1,128)S(1)}, u32[]{:S(2)}, u32[]{:S(2)}) async-start(s32[64,1,8]{2,1,0:T(1,128)} %broadcast_in_dim.124), calls=%async_computation.5 | async-start | bytes 65536 | tf_op jit(solution)/shard_map/all_to_all | solution.py:13
  37.0 31.1 %copy-start.2 = (f32[2048]{0:T(1024)S(1)}, f32[2048]{0:T(1024)}, u32[]{:S(2)}) copy-start(f32[2048]{0:T(1024)} %param.20) | copy-start | bytes 24580
  42.5 16.3 %all-to-all-start.2 = ((bf16[128,2,512]{2,1,0:T(2,128)(2,1)}), bf16[128,2,512]{2,1,0:T(2,128)(2,1)S(1)}, u32[]{:S(2)}, u32[]{:S(2)}) async-start(bf16[128,2,512]{2,1,0:T(2,128)(2,1)} %reshape.540), calls=%async_computation.2 | async-start | bytes 524288 | tf_op jit(solution)/shard_map/all_to_all | solution.py:110
  58.8 9.5 %all-to-all-start.6 = ((s32[2,1,512]{2,1,0:T(1,128)}), s32[2,1,512]{2,1,0:T(1,128)S(1)}, u32[]{:S(2)}, u32[]{:S(2)}) async-start(s32[2,1,512]{2,1,0:T(1,128)} %reshape.562), calls=%async_computation.6 | async-start | bytes 8192 | tf_op jit(solution)/shard_map/all_to_all | solution.py:13
  69.8 36.0 %all-to-all-start.3 = ((bf16[64,8,2048]{2,1,0:T(8,128)(2,1)}), bf16[64,8,2048]{2,1,0:T(8,128)(2,1)}, u32[]{:S(2)}, u32[]{:S(2)}) async-start(bf16[64,8,2048]{2,1,0:T(8,128)(2,1)} %broadcast_in_dim.122), calls=%async_computation.3 | async-start | bytes 4194304 | tf_op jit(solution)/shard_map/all_to_all | solution.py:13
  107.9 8.8 %slice-start = ((s8[8388608]{0:T(1024)(128)(4,1)}), s8[4194304]{0:T(1024)(128)(4,1)S(1)}, s32[]{:S(2)}) async-start(s8[8388608]{0:T(1024)(128)(4,1)} %bitcast.124), calls=%async_computation.7 | async-start | bytes 8388608
  116.1 2.2 %slice-start.1 = ((s8[8388608]{0:T(1024)(128)(4,1)}), s8[4194304]{0:T(1024)(128)(4,1)S(1)}, s32[]{:S(2)}) async-start(s8[8388608]{0:T(1024)(128)(4,1)} %bitcast.124), calls=%async_computation.8 | async-start | bytes 8388608
where the time goes:
time: 168 us
  blocking collectives  51.2 us (30%)
  waiting for transfers between devices  48.4 us (29%)
  starting transfers between devices  31.5 us (19%)
  matrix products  16.1 us (10%)
  local copies, waits for them, and re-layouts  12.8 us (8%)
  other arithmetic  5.45 us (3%)
  between operations  2.23 us (1%)
    all_to_all x4, waiting for transfers between devices, copy_for_each(): lax.all_to_all(jnp.broadcast_to(value[None], (length, *value.shape)), axi...  38.1 us
    all_gather x4, blocking collectives, collected_together(): both, at, found = (lax.all_gather(jnp.concatenate(lines), axis), 0, {})  37.6 us
    all_to_all x4, starting transfers between devices, copy_for_each(): lax.all_to_all(jnp.broadcast_to(value[None], (length, *value.shape)), axi...  26.2 us
    all_to_all x2, blocking collectives, copy_for_each(): lax.all_to_all(jnp.broadcast_to(value[None], (length, *value.shape)), axi...  13.6 us
    dot_general x1, matrix products, per_device(): lax.dot_general(states, embedding, (((1,), (1,)), ((), ())), preferred_el...  10.4 us
    all_to_all x1, waiting for transfers between devices, per_device(): lax.all_to_all(packed, VOCAB, split_axis=0, concat_axis=0, tiled=True)  10.3 us
    broadcast_in_dim x6, local copies, waits for them, and re-layouts, copy_for_each(): jnp.broadcast_to(value[None], (length, *value.shape))  6.46 us
    all_to_all x1, starting transfers between devices, per_device(): lax.all_to_all(packed, VOCAB, split_axis=0, concat_axis=0, tiled=True)  5.31 us
  transfers between devices with their start and end apart: 5, of which 4 were waited for; matrix products, arithmetic and copies ran while one was open for 8% of the time, Pallas kernels for 0%

commit v1 on v0

v1 whole, which is shorter than its diff:
```python
import jax
import jax.numpy as jnp
from jax import lax
from jax.experimental import pallas as pl
from jax.experimental.pallas import tpu as pltpu
from jax.sharding import PartitionSpec as P

MESH = pl.DeviceIdType.MESH
CHIPS = 64
DRAFT = 8
VOC = 2048
D = 2048
PLE = 256
BLOCK = 256
PARTS = ((0, 768), (768, 640), (1408, 640))
ORDERS = ((0, 1, 2), (1, 2, 0), (2, 0, 1))


def kernel(
    ids_s,
    targets_s,
    len_s,
    acc_s,
    hidden_ref,
    post_ref,
    final_ref,
    table_hbm,
    gate_hbm,
    outp_hbm,
    emb_hbm,
    tok_ref,
    seq_ref,
    emb_v,
    table_v,
    gate_v,
    outp_v,
    msg,
    inbox,
    lookup,
    packed,
    arrived,
    gath,
    states,
    even,
    odd,
    res_out,
    res_in,
    load_sem,
    pair_send,
    pair_recv,
    id_sem,
    row_sem,
    res_sem,
    send_sem,
    recv_sem,
):
    me = lax.axis_index("vocab")
    core = me % 2
    chip = me // 2
    sibling = me + 1 - 2 * core
    where_am_i = (chip // 16, (chip // 4) % 4, chip % 4)

    def plane(step):
        return ((chip + step) % CHIPS) * 2 + core

    barrier = pltpu.get_barrier_semaphore()

    def greet(step, carry):
        pl.semaphore_signal(barrier, inc=1, device_id=(plane(step),), device_id_type=MESH)
        return carry

    lax.fori_loop(1, CHIPS, greet, 0)
    pl.semaphore_signal(barrier, inc=1, device_id=(sibling,), device_id_type=MESH)

    loads = [
        pltpu.make_async_copy(gate_hbm, gate_v, load_sem.at[0]),
        pltpu.make_async_copy(outp_hbm, outp_v, load_sem.at[1]),
        pltpu.make_async_copy(table_hbm, table_v.at[core], load_sem.at[2]),
        pltpu.make_async_copy(emb_hbm, emb_v.at[core], load_sem.at[3]),
    ]
    for load in loads:
        load.start()

    ids = [ids_s[0, j] for j in range(DRAFT)]
    lane = lax.broadcasted_iota(jnp.int32, (1, 128), 1)
    id_row = jnp.zeros((1, 128), jnp.int32)
    target_row = jnp.zeros((1, 128), jnp.int32)
    for j in range(DRAFT):
        id_row = jnp.where(lane == j, ids[j], id_row)
        target_row = jnp.where(lane % DRAFT == j, targets_s[0, j], target_row)
    msg[0:1, 0:128] = id_row
    msg[0:1, 128:256] = target_row
    inbox[chip, 0:1, 0:128] = id_row
    inbox[chip, 0:1, 128:256] = target_row

    state = hidden_ref[0]
    loads[0].wait()
    first_gate = jnp.dot(state, gate_v[0], preferred_element_type=jnp.float32)

    pl.semaphore_wait(barrier, CHIPS)

    def send_ids(step, carry):
        pltpu.make_async_remote_copy(
            src_ref=msg,
            dst_ref=inbox.at[chip],
            send_sem=id_sem.at[0],
            recv_sem=id_sem.at[1],
            device_id=(plane(step),),
            device_id_type=MESH,
        ).start()
        return carry

    lax.fori_loop(1, CHIPS, send_ids, 0)
    pair = [
        pltpu.make_async_remote_copy(
            src_ref=source,
            dst_ref=target.at[core],
            send_sem=pair_send.at[k],
            recv_sem=pair_recv.at[k],
            device_id=(sibling,),
            device_id_type=MESH,
        )
        for k, (source, target) in enumerate(((table_hbm, table_v), (emb_hbm, emb_v)))
    ]
    for copy in pair:
        copy.start()

    most = pl.ds(0, CHIPS - 1)

    def wait_all(ref, sem):
        pltpu.make_async_copy(ref.at[most], ref.at[most], sem).wait()

    wait_all(inbox, id_sem.at[1])
    everyone = inbox[:, 0, :]

    all_ids = everyone[:, 0:128]
    lanes = lax.broadcasted_iota(jnp.int32, (CHIPS, 128), 1)
    far = DRAFT * VOC
    voc_lane = lax.broadcasted_iota(jnp.int32, (2 * CHIPS, VOC), 1)
    loads[2].wait()
    pair[0].wait_recv()
    for block in range(2):
        local = all_ids - (chip * 2 + block) * VOC
        hit = (lanes < DRAFT) & (local >= 0) & (local < VOC)
        key = lanes * VOC + local
        first = jnp.min(jnp.where(hit, key, far).astype(jnp.float32), axis=1, keepdims=True)
        last = jnp.max(jnp.where(hit, key, -1).astype(jnp.float32), axis=1, keepdims=True)
        one = jnp.where(first < far, first.astype(jnp.int32) & (VOC - 1), -1)
        two = jnp.where(last > first, last.astype(jnp.int32) & (VOC - 1), -1)
        wanted = jnp.concatenate([one, two], axis=0)
        onehot = jnp.where(voc_lane == wanted, 1.0, 0.0).astype(jnp.bfloat16)
        rows = jnp.dot(onehot, table_v[block], preferred_element_type=jnp.float32)
        for slot in range(2):
            for quarter in range(4):
                lookup[pl.ds((block * 2 + slot) * 4 + quarter, CHIPS, stride=16), :] = rows[
                    slot * CHIPS : (slot + 1) * CHIPS, quarter * 128 : (quarter + 1) * 128
                ]
    packed[...] = lookup[...].astype(jnp.bfloat16).reshape(CHIPS, 16, 128)

    def send_rows(step, carry):
        to = (chip + step) % CHIPS
        pltpu.make_async_remote_copy(
            src_ref=packed.at[to],
            dst_ref=arrived.at[chip],
            send_sem=row_sem.at[0],
            recv_sem=row_sem.at[1],
            device_id=(to * 2 + core,),
            device_id_type=MESH,
        ).start()
        return carry

    lax.fori_loop(1, CHIPS, send_rows, 0)
    arrived[chip] = packed[chip]

    sub = lax.broadcasted_iota(jnp.int32, (32, 1), 0)
    holders = [ids[j] // VOC for j in range(DRAFT)]
    place = jnp.zeros((32, 1), jnp.int32)
    for j in range(DRAFT):
        again = jnp.int32(0)
        for i in range(j):
            again = again | (holders[i] == holders[j]).astype(jnp.int32)
        start = holders[j] * 8 + again * 4
        place = jnp.where(sub % DRAFT == j, start, place)
    place = jnp.where(sub % DRAFT < len_s[0], place + sub // DRAFT, -1)
    slots = lax.broadcasted_iota(jnp.int32, (32, CHIPS * 16), 1)
    picker = jnp.where(slots == place, 1.0, 0.0).astype(jnp.bfloat16)
    wait_all(arrived, row_sem.at[1])
    quarters = jnp.dot(
        picker, arrived[...].reshape(CHIPS * 16, 128), preferred_element_type=jnp.float32
    )
    ple = jnp.concatenate([quarters[8 * q : 8 * q + 8] for q in range(4)], axis=1)

    loads[1].wait()
    for layer in range(2):
        if layer == 0:
            gate = first_gate
        else:
            gate = jnp.dot(state, gate_v[layer], preferred_element_type=jnp.float32)
        gated = jax.nn.gelu(gate, approximate=True)
        gated = (gated * ple[:, layer * PLE : (layer + 1) * PLE]).astype(jnp.bfloat16)
        branch = jnp.dot(gated, outp_v[layer], preferred_element_type=jnp.float32)
        scale = lax.rsqrt(jnp.mean(branch * branch, axis=-1, keepdims=True) + 1e-06)
        state = (
            state.astype(jnp.float32) + post_ref[layer : layer + 1, :] * (branch * scale)
        ).astype(jnp.bfloat16)
    wide = state.astype(jnp.float32)
    scale = lax.rsqrt(jnp.mean(wide * wide, axis=-1, keepdims=True) + 1e-06)
    normed = (final_ref[...].reshape(1, D) * (wide * scale)).astype(jnp.bfloat16)
    gath[where_am_i[0], where_am_i[1], where_am_i[2]] = normed

    sent = []

    def view(part, index):
        start, size = PARTS[part]
        return gath.at[index[0], index[1], index[2], :, pl.ds(start, size)]

    def towards(axis, step):
        place = list(where_am_i)
        place[axis] = (place[axis] + step) % 4
        return (((place[0] * 4 + place[1]) * 4 + place[2]) * 2 + core,)

    def send(part, index, axis, step, slot):
        copy = pltpu.make_async_remote_copy(
            src_ref=view(part, index),
            dst_ref=view(part, index),
            send_sem=send_sem.at[len(sent)],
            recv_sem=recv_sem.at[part, slot],
            device_id=towards(axis, step),
            device_id_type=MESH,
        )
        copy.start()
        sent.append(copy)

    def arrival(part, index, slot):
        ref = view(part, index)
        pltpu.make_async_copy(ref, ref, recv_sem.at[part, slot]).wait()

    def slab(part, level, half=None, shift=0):
        order = ORDERS[part]
        index = list(where_am_i)
        for k in range(level):
            index[order[k]] = pl.ds(0, 4)
        if half is not None:
            index[order[0]] = pl.ds(2 * half, 2)
        index[order[level]] = (index[order[level]] + shift) % 4
        return tuple(index)

    for part in range(3):
        for k, step in enumerate((2, 1, 3)):
            send(part, where_am_i, ORDERS[part][0], step, k)
    for level in (1, 2):
        base = 3 + 4 * (level - 1)
        for part in range(3):
            axis = ORDERS[part][level]
            if level == 1:
                for k in range(3):
                    arrival(part, where_am_i, k)
            else:
                arrival(part, slab(part, 1, 0), base - 2)
                arrival(part, slab(part, 1, 1), base - 1)
            send(part, slab(part, level), axis, 1, base)
            send(part, slab(part, level), axis, 3, base + 1)
        for part in range(3):
            axis = ORDERS[part][level]
            arrival(part, slab(part, level, None, 3), base)
            send(part, slab(part, level, 0, 3), axis, 1, base + 2)
            arrival(part, slab(part, level, None, 1), base + 1)
            send(part, slab(part, level, 1, 1), axis, 3, base + 3)
    for part in range(3):
        arrival(part, slab(part, 2, 0), 9)
        arrival(part, slab(part, 2, 1), 10)

    states[...] = gath[...].reshape(CHIPS * DRAFT, D)
    own_lane = lane // DRAFT
    sub16 = lax.broadcasted_iota(jnp.int32, (16, 128), 0)
    targets = jnp.concatenate(
        [
            jnp.sum(
                jnp.where(
                    sub16 == own_lane, everyone[16 * k : 16 * k + 16, 128:256], 0
                ).astype(jnp.float32),
                axis=0,
                keepdims=True,
            )
            for k in range(4)
        ],
        axis=1,
    ).astype(jnp.int32) - chip * (2 * VOC)
    row = lax.broadcasted_iota(jnp.int32, (BLOCK, CHIPS * DRAFT), 0)

    def fold(value):
        return jnp.sum(value.reshape(BLOCK // 8, 8, CHIPS * DRAFT), axis=0)

    def product(index, out):
        block = emb_v[index // (VOC // BLOCK), pl.ds((index % (VOC // BLOCK)) * BLOCK, BLOCK), :]
        out[...] = lax.dot_general(
            block, states[...], (((1,), (1,)), ((), ())), preferred_element_type=jnp.float32
        )

    def totals(index, out, carry):
        total, picked = carry
        capped = jnp.tanh(out[...] * (1.0 / 30.0)) * 30.0
        total = total + fold(jnp.exp(capped))
        picked = picked + fold(jnp.where(row + index * BLOCK == targets, capped, 0.0))
        return total, picked

    loads[3].wait()
    pair[1].wait_recv()
    zero = jnp.zeros((8, CHIPS * DRAFT), jnp.float32)
    product(0, even)

    def step(k, carry):
        product(2 * k + 1, odd)
        carry = totals(2 * k, even, carry)
        product(2 * k + 2, even)
        return totals(2 * k + 1, odd, carry)

    blocks = 2 * VOC // BLOCK
    carry = lax.fori_loop(0, blocks // 2 - 1, step, (zero, zero))
    product(blocks - 1, odd)
    carry = totals(blocks - 2, even, carry)
    total, picked = totals(blocks - 1, odd, carry)
    total = jnp.sum(total, axis=0, keepdims=True)
    picked = jnp.sum(picked, axis=0, keepdims=True)
    for k in range(4):
        res_out[k, 0:1, :] = total[:, 128 * k : 128 * k + 128]
        res_out[k, 1:2, :] = picked[:, 128 * k : 128 * k + 128]

    def send_results(step, carry):
        to = (chip + step) % CHIPS
        pltpu.make_async_remote_copy(
            src_ref=res_out.at[to // 16],
            dst_ref=res_in.at[chip],
            send_sem=res_sem.at[0],
            recv_sem=res_sem.at[1],
            device_id=(to * 2 + core,),
            device_id_type=MESH,
        ).start()
        return carry

    lax.fori_loop(1, CHIPS, send_results, 0)
    res_in[chip] = res_out[chip // 16]

    for copy in sent:
        copy.wait_send()
    for copy in pair:
        copy.wait_send()

    def wait_sent(ref, sem):
        pltpu.make_async_copy(ref, ref, sem).wait()

    wait_sent(inbox.at[most], id_sem.at[0])
    wait_sent(packed.at[most], row_sem.at[0])
    wait_sent(res_in.at[most], res_sem.at[0])
    wait_all(res_in, res_sem.at[1])
    summed = jnp.sum(res_in[...], axis=0)
    summed = pltpu.roll(summed, (128 - (chip % 16) * DRAFT) % 128, 1)
    score = summed[1:2, :] - jnp.log(summed[0:1, :])
    keep = lane < jnp.minimum(jnp.minimum(acc_s[0], len_s[0]), DRAFT)
    score = jnp.where(keep, score, 0.0)
    tok_ref[...] = score[:, 0:DRAFT]
    seq_ref[0] = jnp.sum(score)


def per_device(
    draft_ids,
    draft_len,
    accepted,
    targets,
    hidden,
    ple_table,
    gate_proj,
    out_proj,
    post_gain,
    final_gain,
    embedding,
):
    smem = pl.BlockSpec(memory_space=pltpu.SMEM)
    vmem = pl.BlockSpec(memory_space=pltpu.VMEM)
    hbm = pl.BlockSpec(memory_space=pl.ANY)
    tokens = CHIPS * DRAFT
    return pl.pallas_call(
        kernel,
        out_shape=(
            jax.ShapeDtypeStruct((1, DRAFT), jnp.float32),
            jax.ShapeDtypeStruct((1,), jnp.float32),
        ),
        in_specs=[smem] * 4 + [vmem] * 3 + [hbm] * 4,
        out_specs=(vmem, smem),
        scratch_shapes=[
            pltpu.VMEM((2, VOC, D), jnp.bfloat16),
            pltpu.VMEM((2, VOC, 2 * PLE), jnp.bfloat16),
            pltpu.VMEM((2, D, PLE), jnp.bfloat16),
            pltpu.VMEM((2, PLE, D), jnp.bfloat16),
            pltpu.VMEM((1, 256), jnp.int32),
            pltpu.VMEM((CHIPS, 1, 256), jnp.int32),
            pltpu.VMEM((CHIPS * 16, 128), jnp.float32),
            pltpu.VMEM((CHIPS, 16, 128), jnp.bfloat16),
            pltpu.VMEM((CHIPS, 16, 128), jnp.bfloat16),
            pltpu.VMEM((4, 4, 4, DRAFT, D), jnp.bfloat16),
            pltpu.VMEM((tokens, D), jnp.bfloat16),
            pltpu.VMEM((BLOCK, tokens), jnp.float32),
            pltpu.VMEM((BLOCK, tokens), jnp.float32),
            pltpu.VMEM((4, 2, 128), jnp.float32),
            pltpu.VMEM((CHIPS, 2, 128), jnp.float32),
            pltpu.SemaphoreType.DMA((4,)),
            pltpu.SemaphoreType.DMA((2,)),
            pltpu.SemaphoreType.DMA((2,)),
            pltpu.SemaphoreType.DMA((2,)),
            pltpu.SemaphoreType.DMA((2,)),
            pltpu.SemaphoreType.DMA((2,)),
            pltpu.SemaphoreType.DMA((33,)),
            pltpu.SemaphoreType.DMA((3, 11)),
        ],
        compiler_params=pltpu.CompilerParams(
            collective_id=0, has_side_effects=True, vmem_limit_bytes=60 * 1024 * 1024
        ),
        name="verify",
    )(
        draft_ids,
        targets,
        draft_len,
        accepted,
        hidden,
        post_gain,
        final_gain,
        ple_table,
        gate_proj,
        out_proj,
        embedding,
    )


def solution(mesh):
    one, two, three = P("vocab"), P("vocab", None), P("vocab", None, None)
    return jax.shard_map(
        per_device,
        mesh=mesh,
        in_specs=(two, one, one, two, three, two, P(), P(), P(), P(), two),
        out_specs=(two, one),
        check_vma=False,
    )
```

time: 168 us -> 70.6 us (0.42)
  the two profiles are of different devices: /device:TPU:1 before, /device:TPU:0 now
where the time goes in v1:
time: 70.6 us; the launch traced here: 70.4 us
  Pallas kernels  65.6 us (93%)
  between operations  3.7 us (5%)
  local copies, waits for them, and re-layouts  1.11 us (2%)
    pallas_call x1, Pallas kernels, per_device(): pl.pallas_call(kernel, out_shape=(jax.ShapeDtypeStruct((1, DRAFT), jnp.fl...  65.6 us

profile of v1, /device:TPU:0, one launch (start us, length us, event | category | flops | bytes accessed | tf_op | source)
XLA Modules:
  0.0 70.4 jit_solution(11635397512794986942)
XLA Ops:
  1.9 65.6 %verify.1 = (f32[1,8]{1,0:T(1,128)}, f32[1]{0:T(128)}) custom-call(s32[1,8]{1,0:T(1,128)} %ids_s.1, s32[1,8]{1,0:T(1,128)} %targets_s.1, s32[1]{0:T(128)S(6)} %copy.15.len_s, s32[1]{0:T(128)S(6)} %copy.16.acc_s, bf16[1,8,2048]{2,1,0:T(8,128)(2,1)} %hidden_ref.1, f32[2,2048]{1,0:T(2,128)} %post_ref.1, f32[2048]{0:T(1024)} %final_ref.1, ...), custom_call_target="tpu_custom_call" | custom-call | tf_op jit(solution)/shard_map/verify/pallas_call | solution.py:382
  67.5 1.1 %copy.17 = f32[1,8]{1,0:T(1,128)} copy(f32[1,8]{1,0:T(1,128)} %get-tuple-element.4) | data formatting | bytes 64
